TPU v7x, 32 devices: a whole 2x2x4 slice. The times are simulated.
32 devices in a mesh: rep: 4 (over y, x), shard: 8 (over z, core).
Axes of the slice: x: 2, y: 2, z: 4, core: 2. Of those that a mesh axis runs over, the one named last changes fastest.
Arguments:
- hot_ids: int32 [65536], P(('rep', 'shard')), may hold values from 0 to 8191
- hot_grads: bfloat16 [65536, 128], P(('rep', 'shard')), may hold values from -6 to 6
- hot_rows: float32 [8192, 128], replicated, may hold values from -6 to 6
- hot_accum: float32 [8192], replicated, may hold values from 0.5 to 4
- cold_counts: int32 [32, 32], P(('rep', 'shard')), may hold values from 1 to 16, as said below
- cold_slots: int32 [32, 32, 16], P(('rep', 'shard')), may hold values from 0 to 8191
- cold_grads: bfloat16 [32, 32, 16, 128], P(('rep', 'shard')), may hold values from -6 to 6
- cold_rows: float32 [262144, 128], P(('rep', 'shard')), may hold values from -6 to 6
- cold_accum: float32 [262144], P(('rep', 'shard')), may hold values from 0.5 to 4
Outputs:
- new_hot_rows: float32 [8192, 128], replicated
- new_hot_accum: float32 [8192], replicated
- new_cold_rows: float32 [262144, 128], P(('rep', 'shard'))
- new_cold_accum: float32 [262144], P(('rep', 'shard'))
Inputs may be any that keep to these rules, and one draw needn't show every extreme that they name: `cold_counts`: every entry is at least 1 and at most 16; in every draw some owner receives 16 live slots from every sender.
All inputs are finite; a program needn't handle non-finite values.
Results may differ from a plain program's by a relative error of at most 0.0003.
Values may be sent and summed in bfloat16 or wider, within the bound.
A program may use at most 128 MiB of HBM per device.

v0:
```python
import jax
import jax.numpy as jnp
from jax import lax
from jax.sharding import PartitionSpec as P

learn_rate = 0.5


def adagrad(table_rows, accum_rows, gradient):
    accum_new = accum_rows + jnp.mean(gradient * gradient, axis=1)
    return (table_rows - learn_rate * gradient / jnp.sqrt(accum_new)[:, None], accum_new)


def local(
    hot_ids,
    hot_grads,
    hot_rows,
    hot_accum,
    cold_counts,
    cold_slots,
    cold_grads,
    cold_rows,
    cold_accum,
):
    hot_count = hot_rows.shape[0]
    dense = jax.ops.segment_sum(hot_grads.astype(jnp.float32), hot_ids, num_segments=hot_count)
    share = hot_count // lax.axis_size("shard")
    part_sum = lax.psum_scatter(dense, "shard", scatter_dimension=0, tiled=True)
    part_sum = lax.psum(part_sum, "rep")
    start = lax.axis_index("shard") * share
    rows_share = lax.dynamic_slice_in_dim(hot_rows, start, share, 0)
    accum_share = lax.dynamic_slice_in_dim(hot_accum, start, share, 0)
    rows_new, accum_new = adagrad(rows_share, accum_share, part_sum)
    new_hot_rows, new_hot_accum = (
        lax.all_gather(rows_new, "shard", axis=0, tiled=True),
        lax.all_gather(accum_new, "shard", axis=0, tiled=True),
    )
    received, slots_in, counts_in = (
        lax.all_to_all(cold_grads, ("rep", "shard"), split_axis=1, concat_axis=0, tiled=True),
        lax.all_to_all(cold_slots, ("rep", "shard"), split_axis=1, concat_axis=0, tiled=True),
        lax.all_to_all(cold_counts, ("rep", "shard"), split_axis=1, concat_axis=0, tiled=True),
    )
    width = received.shape[-1]
    capacity = received.shape[2]
    slot_index = lax.broadcasted_iota(jnp.int32, (1, 1, capacity), 2)
    live_mask = slot_index < counts_in[:, :, None]
    masked_terms = jnp.where(live_mask[..., None], received.astype(jnp.float32), 0.0)
    local_rows = cold_rows.shape[0]
    cold_sum = jax.ops.segment_sum(
        masked_terms.reshape(-1, width), slots_in.reshape(-1), num_segments=local_rows
    )
    new_cold_rows, new_cold_accum = adagrad(cold_rows, cold_accum, cold_sum)
    return (new_hot_rows, new_hot_accum, new_cold_rows, new_cold_accum)


def solution(mesh):
    placed = (
        P(("rep", "shard")),
        P(("rep", "shard"), None),
        P(),
        P(),
        P(("rep", "shard"), None),
        P(("rep", "shard"), None, None),
        P(("rep", "shard"), None, None, None),
        P(("rep", "shard"), None),
        P(("rep", "shard")),
    )
    return jax.shard_map(
        local,
        mesh=mesh,
        in_specs=placed,
        out_specs=(P(), P(), P(("rep", "shard"), None), P(("rep", "shard"))),
        check_vma=False,
    )
```

profile of v0, /device:TPU:0, one launch (start us, length us, event | category | flops | bytes accessed | tf_op | source)
XLA Modules:
  0.0 199.6 jit_solution(5830766798041887270)
XLA Ops:
  7.2 0.0 reduce-scatter.2.cloned.1.call-start
  7.2 14.1 %scatter_custom_fusion = f32[8192,128]{1,0:T(8,128)} fusion(s32[2048]{0:T(1024)} %param.9, f32[]{:T(128)} %constant.3.clone.1, bf16[2048,128]{1,0:T(8,128)(2,1)} %param.10), kind=kCustom, calls=%fused_computation.6 | custom fusion | flops 524288 | bytes 4719104 | tf_op jit(solution)/shard_map/scatter-add | solution.py:26
  21.3 0.0 copy-start.3
  21.3 0.0 copy-start.2
  21.3 0.0 reduce-scatter.2.cloned.1.call-update
  21.3 0.0 all-reduce.2.cloned.1.call-start
  21.4 52.8 %reduce-scatter.2.cloned.1.call-done = f32[1024,128]{1,0:T(8,128)} async-done(((f32[8192,128]{1,0:T(8,128)}), f32[1024,128]{1,0:T(8,128)}) %reduce-scatter.2.cloned.1.call-update) | async-done | bytes 524304 | tf_op jit(solution)/shard_map/reduce_scatter | solution.py:28
  74.1 0.0 all-reduce.2.cloned.1.call-update
  74.2 0.0 all-gather.2.cloned.1.call-start
  74.2 46.8 %all-reduce.2.cloned.1.call-done = f32[1024,128]{1,0:T(8,128)} async-done(((f32[1024,128]{1,0:T(8,128)}), f32[1024,128]{1,0:T(8,128)}) %all-reduce.2.cloned.1.call-update) | async-done | bytes 524304 | tf_op jit(solution)/shard_map/psum | solution.py:29
  121.0 1.2 multiply_reduce_fusion.1
  122.2 0.7 fusion.8
  122.9 2.2 %divide_subtract_fusion.1 = f32[1024,128]{1,0:T(8,128)} fusion(f32[1024,128]{1,0:T(8,128)} %all-reduce.2.cloned.1.call-done, f32[8192,128]{1,0:T(8,128)} %param.11, s32[]{:T(128)S(6)} %select_n.11, f32[1024]{0:T(1024)S(1)} %get-tuple-element.6), kind=kLoop, calls=%fused_computation.9 | loop fusion | flops 393216 | bytes 1576964 | tf_op jit(solution)/shard_map/sub | solution.py:11
  125.1 0.0 all-gather.2.cloned.1.call-update
  125.2 0.0 copy-done.3
  125.2 0.7 copy.18
  125.9 4.6 %all-to-all-start.1 = ((s32[1,32,1]{2,0,1:T(1,128)}), s32[1,32,1]{2,0,1:T(1,128)S(1)}, u32[]{:S(2)}, u32[]{:S(2)}) async-start(s32[1,32,1]{2,0,1:T(1,128)} %copy.18), calls=%async_computation.2 | async-start | bytes 32768 | tf_op jit(solution)/shard_map/all_to_all | solution.py:41
  130.5 0.0 copy-done.2
  130.5 0.1 copy.17
  130.6 7.0 %all-to-all-done.1 = s32[1,32,1]{2,0,1:T(1,128)S(1)} async-done(((s32[1,32,1]{2,0,1:T(1,128)}), s32[1,32,1]{2,0,1:T(1,128)S(1)}, u32[]{:S(2)}, u32[]{:S(2)}) %all-to-all-start.1) | async-done | bytes 160 | tf_op jit(solution)/shard_map/all_to_all | solution.py:41
  137.6 9.1 %all_to_all.31 = s32[1,32,16]{2,0,1:T(1,128)S(1)} all-to-all(s32[1,32,16]{2,0,1:T(1,128)S(1)} %copy.17), channel_id=1, replica_groups=mesh['rep'=4,'shard'=8] {'rep','shard'}, dimensions={1} | all-to-all | bytes 4096 | tf_op jit(solution)/shard_map/all_to_all | solution.py:40
  146.7 2.6 %all-to-all-start.2 = ((bf16[1,32,16,128]{3,2,0,1:T(8,128)(2,1)}), bf16[1,32,16,128]{3,2,0,1:T(8,128)(2,1)S(1)}, u32[]{:S(2)}, u32[]{:S(2)}) async-start(bf16[1,32,16,128]{3,2,0,1:T(8,128)(2,1)} %bitcast.1), calls=%async_computation.3 | async-start | bytes 262144 | tf_op jit(solution)/shard_map/all_to_all | solution.py:39
  149.3 0.7 reduce.1
  150.0 0.1 iota_compare_fusion
  150.0 0.1 lt.33
  150.1 0.5 broadcast.40
  150.6 0.7 reduce.4
  151.3 0.1 reshape.77
  151.4 9.5 %all-to-all-done.2 = bf16[1,32,16,128]{3,2,0,1:T(8,128)(2,1)S(1)} async-done(((bf16[1,32,16,128]{3,2,0,1:T(8,128)(2,1)}), bf16[1,32,16,128]{3,2,0,1:T(8,128)(2,1)S(1)}, u32[]{:S(2)}, u32[]{:S(2)}) %all-to-all-start.2) | async-done | bytes 131104 | tf_op jit(solution)/shard_map/all_to_all | solution.py:39
  160.9 0.0 copy-start.1
  160.9 4.6 %scatter_custom_fusion.1 = f32[8192,128]{1,0:T(8,128)} fusion(s32[512]{0:T(512)S(1)} %reshape.77, f32[]{:T(128)} %constant.3.clone.1, bf16[512,128]{1,0:T(8,128)(2,1)S(1)} %bitcast.7, pred[512]{0:T(512)(128)(4,1)S(1)} %lt.33), kind=kCustom, calls=%fused_computation.4 | custom fusion | flops 196608 | bytes 4326912 | tf_op jit(solution)/shard_map/scatter-add | solution.py:49
  165.5 0.0 copy-start
  165.5 3.5 %multiply_reduce_fusion = f32[8192]{0:T(1024)S(1)} fusion(f32[8192,128]{1,0:T(8,128)} %scatter_custom_fusion.1), kind=kLoop, calls=%fused_computation.3 | loop fusion | flops 2088960 | bytes 4227072 | tf_op jit(solution)/shard_map/reduce_sum | solution.py:10
  169.0 0.0 copy-done.1
  169.1 0.6 fusion.7
  169.7 0.0 copy-done
  169.7 4.2 %divide_subtract_fusion = f32[8192,128]{1,0:T(8,128)} fusion(f32[8192,128]{1,0:T(8,128)} %param.16, f32[8192,128]{1,0:T(8,128)S(1)} %copy-done, f32[8192]{0:T(1024)S(1)} %get-tuple-element.4), kind=kLoop, calls=%fused_computation.2 | loop fusion | flops 3145728 | bytes 12615680 | tf_op jit(solution)/shard_map/sub | solution.py:11
  173.9 14.1 %all_gather.7 = f32[8192]{0:T(1024)S(1)} all-gather(f32[1024]{0:T(1024)S(1)} %get-tuple-element.7), channel_id=1, replica_groups=mesh['rep'=4,'shard'=8] {'shard'}, dimensions={0}, use_global_device_ids=true | all-gather | bytes 36864 | tf_op jit(solution)/shard_map/all_gather | solution.py:36
  188.0 0.0 all-gather.2.cloned.1.call-done
  188.0 4.5 %copy.23 = f32[8192,128]{1,0:T(8,128)} copy(f32[8192,128]{1,0:T(8,128)} %all-gather.2.cloned.1.call-done) | data formatting | bytes 8388608
  192.4 0.6 copy.24
Async XLA Ops:
  7.2 67.0 %reduce-scatter.2.cloned.1.call-start = ((), (), s32[]{:S(2)}) async-start(), calls=%async_computation.4 | async-start | bytes 4718592 | tf_op jit(solution)/shard_map/reduce_scatter | solution.py:28
  21.3 103.9 %copy-start.3 = (s32[1,32]{1,0:T(1,128)S(1)}, s32[1,32]{1,0:T(1,128)}, u32[]{:S(2)}) copy-start(s32[1,32]{1,0:T(1,128)} %param.13) | copy-start | bytes 388
  21.3 109.2 %copy-start.2 = (s32[1,32,16]{1,2,0:T(8,128)S(1)}, s32[1,32,16]{1,2,0:T(8,128)}, u32[]{:S(2)}) copy-start(s32[1,32,16]{1,2,0:T(8,128)} %param.14) | copy-start | bytes 6148
  21.3 99.7 %all-reduce.2.cloned.1.call-start = ((), (), s32[]{:S(2)}) async-start(), calls=%async_computation.5 | async-start | bytes 1048576 | tf_op jit(solution)/shard_map/psum | solution.py:29
  74.2 113.8 %all-gather.2.cloned.1.call-start = ((), (), s32[]{:S(2)}) async-start(), calls=%async_computation.6 | async-start | bytes 4718592 | tf_op jit(solution)/shard_map/all_gather | solution.py:35
  125.9 11.7 %all-to-all-start.1 = ((s32[1,32,1]{2,0,1:T(1,128)}), s32[1,32,1]{2,0,1:T(1,128)S(1)}, u32[]{:S(2)}, u32[]{:S(2)}) async-start(s32[1,32,1]{2,0,1:T(1,128)} %copy.18), calls=%async_computation.2 | async-start | bytes 32768 | tf_op jit(solution)/shard_map/all_to_all | solution.py:41
  146.7 14.2 %all-to-all-start.2 = ((bf16[1,32,16,128]{3,2,0,1:T(8,128)(2,1)}), bf16[1,32,16,128]{3,2,0,1:T(8,128)(2,1)S(1)}, u32[]{:S(2)}, u32[]{:S(2)}) async-start(bf16[1,32,16,128]{3,2,0,1:T(8,128)(2,1)} %bitcast.1), calls=%async_computation.3 | async-start | bytes 262144 | tf_op jit(solution)/shard_map/all_to_all | solution.py:39
  160.9 8.1 %copy-start.1 = (f32[8192]{0:T(1024)S(1)}, f32[8192]{0:T(1024)}, u32[]{:S(2)}) copy-start(f32[8192]{0:T(1024)} %param.17) | copy-start | bytes 98308
  165.5 4.1 %copy-start = (f32[8192,128]{1,0:T(8,128)S(1)}, f32[8192,128]{1,0:T(8,128)}, u32[]{:S(2)}) copy-start(f32[8192,128]{1,0:T(8,128)} %scatter_custom_fusion.1) | copy-start | bytes 12582916
Sparse Core Ops, SparseCore 0:
  21.4 52.6 reduce-scatter.1
  77.1 43.8 all-reduce.1
  125.3 50.0 all-gather.1
where the time goes:
time: 200 us
  waiting for transfers between devices  116 us (58%)
  other arithmetic  32.6 us (16%)
  blocking collectives  23.2 us (12%)
  between operations  13.8 us (7%)
  starting transfers between devices  7.29 us (4%)
  local copies, waits for them, and re-layouts  6.56 us (3%)
    reduce_scatter x1, waiting for transfers between devices, local(): part_sum = lax.psum_scatter(dense, 'shard', scatter_dimension=0, tiled=True)  52.8 us
    psum x1, waiting for transfers between devices, local(): part_sum = lax.psum(part_sum, 'rep')  46.8 us
    scatter-add x1, other arithmetic, local(): jax.ops.segment_sum(hot_grads.astype(jnp.float32), hot_ids, num_segments=...  14.1 us
    all_gather x1, blocking collectives, local(): lax.all_gather(accum_new, 'shard', axis=0, tiled=True)  14.1 us
    all_to_all x1, waiting for transfers between devices, local(): lax.all_to_all(cold_grads, ('rep', 'shard'), split_axis=1, concat_axis=0,...  9.51 us
    all_to_all x1, blocking collectives, local(): lax.all_to_all(cold_slots, ('rep', 'shard'), split_axis=1, concat_axis=0,...  9.13 us
    all_to_all x1, waiting for transfers between devices, local(): lax.all_to_all(cold_counts, ('rep', 'shard'), split_axis=1, concat_axis=0...  7.01 us
    sub x2, other arithmetic, adagrad(): table_rows - learn_rate * gradient / jnp.sqrt(accum_new)[:, None]  6.43 us
  transfers between devices with their start and end apart: 5, of which 4 were waited for; matrix products, arithmetic and copies ran while one was open for 8% of the time, Pallas kernels for 0%

commit v1 on v0

--- a/solution.py
+++ b/solution.py
@@ -26,7 +26,7 @@
     dense = jax.ops.segment_sum(hot_grads.astype(jnp.float32), hot_ids, num_segments=hot_count)
     share = hot_count // lax.axis_size("shard")
     part_sum = lax.psum_scatter(dense, "shard", scatter_dimension=0, tiled=True)
-    part_sum = lax.psum(part_sum, "rep")
+    part_sum = jnp.sum(lax.all_gather(part_sum, "rep"), axis=0)
     start = lax.axis_index("shard") * share
     rows_share = lax.dynamic_slice_in_dim(hot_rows, start, share, 0)
     accum_share = lax.dynamic_slice_in_dim(hot_accum, start, share, 0)

time: 200 us -> 189 us (0.945)
  waiting for transfers between devices: 116 us -> 105 us
    psum x1 -> x0, waiting for transfers between devices: 46.8 us -> none  [local(): part_sum = lax.psum(part_sum, 'rep')]
    all_gather x0 -> x1, waiting for transfers between devices: none -> 35.4 us  [local(): part_sum = jnp.sum(lax.all_gather(part_sum, 'rep'), axis=0)]
where the time goes in v1:
time: 189 us
  waiting for transfers between devices  105 us (56%)
  other arithmetic  33.2 us (18%)
  blocking collectives  23.2 us (12%)
  between operations  13.8 us (7%)
  starting transfers between devices  7.29 us (4%)
  local copies, waits for them, and re-layouts  6.56 us (3%)
    reduce_scatter x1, waiting for transfers between devices, local(): part_sum = lax.psum_scatter(dense, 'shard', scatter_dimension=0, tiled=True)  52.8 us
    all_gather x1, waiting for transfers between devices, local(): part_sum = jnp.sum(lax.all_gather(part_sum, 'rep'), axis=0)  35.4 us
    scatter-add x1, other arithmetic, local(): jax.ops.segment_sum(hot_grads.astype(jnp.float32), hot_ids, num_segments=...  14.1 us
    all_gather x1, blocking collectives, local(): lax.all_gather(accum_new, 'shard', axis=0, tiled=True)  14.1 us
    all_to_all x1, waiting for transfers between devices, local(): lax.all_to_all(cold_grads, ('rep', 'shard'), split_axis=1, concat_axis=0,...  9.51 us
    all_to_all x1, blocking collectives, local(): lax.all_to_all(cold_slots, ('rep', 'shard'), split_axis=1, concat_axis=0,...  9.13 us
    all_to_all x1, waiting for transfers between devices, local(): lax.all_to_all(cold_counts, ('rep', 'shard'), split_axis=1, concat_axis=0...  7.02 us
    sub x2, other arithmetic, adagrad(): table_rows - learn_rate * gradient / jnp.sqrt(accum_new)[:, None]  6.27 us
  transfers between devices with their start and end apart: 5, of which 4 were waited for; matrix products, arithmetic and copies ran while one was open for 8% of the time, Pallas kernels for 0%

profile of v1, /device:TPU:0, one launch (start us, length us, event | category | flops | bytes accessed | tf_op | source)
XLA Modules:
  0.0 188.8 jit_solution(13003348099846185917)
XLA Ops:
  7.2 0.0 reduce-scatter.2.cloned.1.call-start
  7.2 14.1 %scatter_custom_fusion = f32[8192,128]{1,0:T(8,128)} fusion(s32[2048]{0:T(1024)} %param.9, f32[]{:T(128)} %constant.3.clone.1, bf16[2048,128]{1,0:T(8,128)(2,1)} %param.10), kind=kCustom, calls=%fused_computation.6 | custom fusion | flops 524288 | bytes 4719104 | tf_op jit(solution)/shard_map/scatter-add | solution.py:26
  21.3 0.0 copy-start.3
  21.3 0.0 copy-start.2
  21.3 0.0 reduce-scatter.2.cloned.1.call-update
  21.3 0.0 all-gather.6.cloned.1.call-start
  21.4 52.8 %reduce-scatter.2.cloned.1.call-done = f32[1024,128]{1,0:T(8,128)} async-done(((f32[8192,128]{1,0:T(8,128)}), f32[1024,128]{1,0:T(8,128)}) %reduce-scatter.2.cloned.1.call-update) | async-done | bytes 524304 | tf_op jit(solution)/shard_map/reduce_scatter | solution.py:28
  74.1 0.0 all-gather.6.cloned.1.call-update
  74.2 0.0 all-gather.4.cloned.1.call-start
  74.2 35.4 %all-gather.6.cloned.1.call-done = f32[4096,128]{1,0:T(8,128)} async-done(((f32[1024,128]{1,0:T(8,128)}), f32[4096,128]{1,0:T(8,128)}) %all-gather.6.cloned.1.call-update) | async-done | bytes 2097168 | tf_op jit(solution)/shard_map/all_gather | solution.py:29
  109.7 1.8 reduce_sum.27
  111.4 0.2 multiply_reduce_fusion.1
  111.6 0.7 fusion.8
  112.3 2.0 %divide_subtract_fusion.1 = f32[1024,128]{1,0:T(8,128)} fusion(f32[1024,128]{1,0:T(8,128)S(1)} %reduce_sum.27, f32[8192,128]{1,0:T(8,128)} %param.11, s32[]{:T(128)S(6)} %select_n.11, f32[1024]{0:T(1024)S(1)} %get-tuple-element.6), kind=kLoop, calls=%fused_computation.9 | loop fusion | flops 393216 | bytes 1576964 | tf_op jit(solution)/shard_map/sub | solution.py:11
  114.4 0.0 all-gather.4.cloned.1.call-update
  114.4 0.0 copy-done.3
  114.4 0.7 copy.18
  115.1 4.6 %all-to-all-start.1 = ((s32[1,32,1]{2,0,1:T(1,128)}), s32[1,32,1]{2,0,1:T(1,128)S(1)}, u32[]{:S(2)}, u32[]{:S(2)}) async-start(s32[1,32,1]{2,0,1:T(1,128)} %copy.18), calls=%async_computation.2 | async-start | bytes 32768 | tf_op jit(solution)/shard_map/all_to_all | solution.py:41
  119.7 0.0 copy-done.2
  119.7 0.1 copy.17
  119.8 7.0 %all-to-all-done.1 = s32[1,32,1]{2,0,1:T(1,128)S(1)} async-done(((s32[1,32,1]{2,0,1:T(1,128)}), s32[1,32,1]{2,0,1:T(1,128)S(1)}, u32[]{:S(2)}, u32[]{:S(2)}) %all-to-all-start.1) | async-done | bytes 160 | tf_op jit(solution)/shard_map/all_to_all | solution.py:41
  126.8 9.1 %all_to_all.31 = s32[1,32,16]{2,0,1:T(1,128)S(1)} all-to-all(s32[1,32,16]{2,0,1:T(1,128)S(1)} %copy.17), channel_id=1, replica_groups=mesh['rep'=4,'shard'=8] {'rep','shard'}, dimensions={1} | all-to-all | bytes 4096 | tf_op jit(solution)/shard_map/all_to_all | solution.py:40
  135.9 2.6 %all-to-all-start.2 = ((bf16[1,32,16,128]{3,2,0,1:T(8,128)(2,1)}), bf16[1,32,16,128]{3,2,0,1:T(8,128)(2,1)S(1)}, u32[]{:S(2)}, u32[]{:S(2)}) async-start(bf16[1,32,16,128]{3,2,0,1:T(8,128)(2,1)} %bitcast.2), calls=%async_computation.3 | async-start | bytes 262144 | tf_op jit(solution)/shard_map/all_to_all | solution.py:39
  138.5 0.7 reduce.1
  139.2 0.1 iota_compare_fusion
  139.3 0.1 lt.33
  139.4 0.5 broadcast.40
  139.9 0.7 reduce.4
  140.6 0.1 reshape.77
  140.7 9.5 %all-to-all-done.2 = bf16[1,32,16,128]{3,2,0,1:T(8,128)(2,1)S(1)} async-done(((bf16[1,32,16,128]{3,2,0,1:T(8,128)(2,1)}), bf16[1,32,16,128]{3,2,0,1:T(8,128)(2,1)S(1)}, u32[]{:S(2)}, u32[]{:S(2)}) %all-to-all-start.2) | async-done | bytes 131104 | tf_op jit(solution)/shard_map/all_to_all | solution.py:39
  150.2 0.0 copy-start.1
  150.2 4.6 %scatter_custom_fusion.1 = f32[8192,128]{1,0:T(8,128)} fusion(s32[512]{0:T(512)S(1)} %reshape.77, f32[]{:T(128)} %constant.3.clone.1, bf16[512,128]{1,0:T(8,128)(2,1)S(1)} %bitcast.9, pred[512]{0:T(512)(128)(4,1)S(1)} %lt.33), kind=kCustom, calls=%fused_computation.4 | custom fusion | flops 196608 | bytes 4326912 | tf_op jit(solution)/shard_map/scatter-add | solution.py:49
  154.8 0.0 copy-start
  154.8 3.5 %multiply_reduce_fusion = f32[8192]{0:T(1024)S(1)} fusion(f32[8192,128]{1,0:T(8,128)} %scatter_custom_fusion.1), kind=kLoop, calls=%fused_computation.3 | loop fusion | flops 2088960 | bytes 4227072 | tf_op jit(solution)/shard_map/reduce_sum | solution.py:10
  158.3 0.0 copy-done.1
  158.3 0.6 fusion.7
  158.9 0.0 copy-done
  158.9 4.2 %divide_subtract_fusion = f32[8192,128]{1,0:T(8,128)} fusion(f32[8192,128]{1,0:T(8,128)} %param.16, f32[8192,128]{1,0:T(8,128)S(1)} %copy-done, f32[8192]{0:T(1024)S(1)} %get-tuple-element.4), kind=kLoop, calls=%fused_computation.2 | loop fusion | flops 3145728 | bytes 12615680 | tf_op jit(solution)/shard_map/sub | solution.py:11
  163.1 14.1 %all_gather.15 = f32[8192]{0:T(1024)S(1)} all-gather(f32[1024]{0:T(1024)S(1)} %get-tuple-element.7), channel_id=1, replica_groups=mesh['rep'=4,'shard'=8] {'shard'}, dimensions={0}, use_global_device_ids=true | all-gather | bytes 36864 | tf_op jit(solution)/shard_map/all_gather | solution.py:36
  177.2 0.0 all-gather.4.cloned.1.call-done
  177.2 4.5 %copy.22 = f32[8192,128]{1,0:T(8,128)} copy(f32[8192,128]{1,0:T(8,128)} %all-gather.4.cloned.1.call-done) | data formatting | bytes 8388608
  181.7 0.6 copy.23
Async XLA Ops:
  7.2 67.0 %reduce-scatter.2.cloned.1.call-start = ((), (), s32[]{:S(2)}) async-start(), calls=%async_computation.4 | async-start | bytes 4718592 | tf_op jit(solution)/shard_map/reduce_scatter | solution.py:28
  21.3 93.1 %copy-start.3 = (s32[1,32]{1,0:T(1,128)S(1)}, s32[1,32]{1,0:T(1,128)}, u32[]{:S(2)}) copy-start(s32[1,32]{1,0:T(1,128)} %param.13) | copy-start | bytes 388
  21.3 98.4 %copy-start.2 = (s32[1,32,16]{1,2,0:T(8,128)S(1)}, s32[1,32,16]{1,2,0:T(8,128)}, u32[]{:S(2)}) copy-start(s32[1,32,16]{1,2,0:T(8,128)} %param.14) | copy-start | bytes 6148
  21.3 88.3 %all-gather.6.cloned.1.call-start = ((), (), s32[]{:S(2)}) async-start(), calls=%async_computation.6 | async-start | bytes 2621440 | tf_op jit(solution)/shard_map/all_gather | solution.py:29
  74.2 103.0 %all-gather.4.cloned.1.call-start = ((), (), s32[]{:S(2)}) async-start(), calls=%async_computation.5 | async-start | bytes 4718592 | tf_op jit(solution)/shard_map/all_gather | solution.py:35
  115.1 11.7 %all-to-all-start.1 = ((s32[1,32,1]{2,0,1:T(1,128)}), s32[1,32,1]{2,0,1:T(1,128)S(1)}, u32[]{:S(2)}, u32[]{:S(2)}) async-start(s32[1,32,1]{2,0,1:T(1,128)} %copy.18), calls=%async_computation.2 | async-start | bytes 32768 | tf_op jit(solution)/shard_map/all_to_all | solution.py:41
  135.9 14.2 %all-to-all-start.2 = ((bf16[1,32,16,128]{3,2,0,1:T(8,128)(2,1)}), bf16[1,32,16,128]{3,2,0,1:T(8,128)(2,1)S(1)}, u32[]{:S(2)}, u32[]{:S(2)}) async-start(bf16[1,32,16,128]{3,2,0,1:T(8,128)(2,1)} %bitcast.2), calls=%async_computation.3 | async-start | bytes 262144 | tf_op jit(solution)/shard_map/all_to_all | solution.py:39
  150.2 8.1 %copy-start.1 = (f32[8192]{0:T(1024)S(1)}, f32[8192]{0:T(1024)}, u32[]{:S(2)}) copy-start(f32[8192]{0:T(1024)} %param.17) | copy-start | bytes 98308
  154.8 4.1 %copy-start = (f32[8192,128]{1,0:T(8,128)S(1)}, f32[8192,128]{1,0:T(8,128)}, u32[]{:S(2)}) copy-start(f32[8192,128]{1,0:T(8,128)} %scatter_custom_fusion.1) | copy-start | bytes 12582916
Sparse Core Ops, SparseCore 0:
  21.4 52.6 reduce-scatter.1
  76.0 33.6 all-gather.5
  114.5 50.0 all-gather.3
